TPU v7x, 32 devices: a whole 2x2x4 slice. The times are simulated.
32 devices in a mesh: cat: 2 (over x), lat: 4 (over y, core), lon: 4 (over z).
Axes of the slice: x: 2, y: 2, z: 4, core: 2. Of those that a mesh axis runs over, the one named last changes fastest.
Arguments:
- thickness: bfloat16 [40, 1024, 2560], P('cat', 'lat', 'lon'), may hold values from 0.099609375 to 4
- area: bfloat16 [40, 1024, 2560], P('cat', 'lat', 'lon'), may hold values from 0.0049743652 to 0.049804688
- ridge_weight: float32 [40], P('cat'), may hold values from 0.2 to 2
- cat_top: int32 [1024, 2560], P('lat', 'lon'), may hold values from 1 to 40
- land_mask: int32 [1024, 2560], P('lat', 'lon'), may hold values 0 or 1
- velocity_u: float32 [1024, 2560], P('lat', 'lon'), may hold values from -1.8 to 1.8
- velocity_v: float32 [1024, 2560], P('lat', 'lon'), may hold values from -1.8 to 1.8
- stress_div: float32 [1024, 2560], P('lat', 'lon'), may hold values from -3 to 3
- stress_ten: float32 [1024, 2560], P('lat', 'lon'), may hold values from -3 to 3
- stress_shear: float32 [1024, 2560], P('lat', 'lon'), may hold values from -3 to 3
- wind_x: float32 [1024, 2560], P('lat', 'lon'), may hold values from -6 to 6
- wind_y: float32 [1024, 2560], P('lat', 'lon'), may hold values from -6 to 6
- water_drag: float32 [1024, 2560], P('lat', 'lon'), may hold values from 0.2 to 2
Outputs:
- new_u: float32 [1024, 2560], P('lat', 'lon')
- new_v: float32 [1024, 2560], P('lat', 'lon')
- new_div: float32 [1024, 2560], P('lat', 'lon')
- new_ten: float32 [1024, 2560], P('lat', 'lon')
- new_shear: float32 [1024, 2560], P('lat', 'lon')
Inputs may be any that keep to these rules, and one draw needn't show every extreme that they name: Categories with index cat_top or above are absent from a cell.
All inputs are finite; a program needn't handle non-finite values. No bound on the sum of `land_mask` on one device may be relied on, other than what follows from the above.
Results may differ from a plain program's by a relative error of at most 0.0003.
Values sent between devices are 32-bit elements; how exact they have to be, the bound alone decides.
A program may use at most 128 MiB of HBM per device.

v0:
```python
import functools

import jax
import jax.numpy as jnp
from jax import lax
from jax.experimental import pallas as pl
from jax.experimental.pallas import tpu as pltpu
from jax.sharding import PartitionSpec as P

SUB = 4
LANES = 128
EDGE = 8
BLOCK = 16
CHUNK = 32
FINAL = 16
TOP = 16
FOLD = 4
MESH = pl.DeviceIdType.MESH

FS, FM, FC, FD, FX, FY, FW, FU, FV, FA, FB, FT = range(12)
FIELDS = 12
THIRD = 1.0 / 3.0


def read(field, f, c, r, shift=0):
    if shift == 0:
        return field[f, c, pl.ds(pl.multiple_of(r, EDGE), EDGE), :]
    near = field.at[f, c, pl.ds(pl.multiple_of(r - EDGE, EDGE), 3 * EDGE)]
    return near[EDGE + shift : 2 * EDGE + shift, :]


def put(ref, value, mask):
    if mask is None:
        ref[...] = value
    else:
        pltpu.store(ref, value, mask=mask)


def along(x, lane):
    tiles = len(x)
    ahead = [pltpu.roll(a, LANES - 1, 1) for a in x]
    behind = [pltpu.roll(a, 1, 1) for a in x]
    return [
        jnp.where(lane == LANES - 1, ahead[(c + 1) % tiles], ahead[c])
        - jnp.where(lane == 0, behind[c - 1], behind[c])
        for c in range(tiles)
    ]


def derive(field, r):
    tiles = field.shape[1]
    at = pl.ds(pl.multiple_of(r, EDGE), EDGE)
    for c in range(tiles):
        wet = field[FW, c, at, :]
        mass = field[FM, c, at, :]
        ratio = wet / (mass + field[FD, c, at, :] + 1.0 - wet)
        force = field[FC, c, at, :] * ratio
        field[FS, c, at, :] = (2.0 * THIRD) * wet * field[FS, c, at, :]
        field[FM, c, at, :] = mass * ratio
        field[FD, c, at, :] = 0.25 * ratio
        field[FX, c, at, :] = force * field[FX, c, at, :]
        field[FY, c, at, :] = force * field[FY, c, at, :]
        field[FW, c, at, :] = THIRD * wet
        first = field[FA, c, at, :]
        second = field[FB, c, at, :]
        field[FA, c, at, :] = first + second
        field[FB, c, at, :] = first - second
        field[FT, c, at, :] = 2.0 * field[FT, c, at, :]


def stress(field, outs, r, mask, lane):
    tiles = field.shape[1]
    at = pl.ds(pl.multiple_of(r, EDGE), EDGE)
    dxu = along([field[FU, c, at, :] for c in range(tiles)], lane)
    dxv = along([field[FV, c, at, :] for c in range(tiles)], lane)
    for c in range(tiles):
        dyu = read(field, FU, c, r, 1) - read(field, FU, c, r, -1)
        dyv = read(field, FV, c, r, 1) - read(field, FV, c, r, -1)
        div = dxu[c] + dyv
        ten = dxu[c] - dyv
        shr = dyu + dxv[c]
        inverse = lax.rsqrt(div * div + 0.25 * (ten * ten + shr * shr) + 0.01)
        power = field[FS, c, at, :]
        keep = field[FW, c, at, :]
        gain = power * inverse
        p = gain * div - power
        q = (0.25 * gain) * ten
        a = keep * field[FA, c, at, :] + (p + q)
        b = keep * field[FB, c, at, :] + (p - q)
        s = keep * field[FT, c, at, :] + (0.5 * gain) * shr
        put(field.at[FA, c, at], a, mask)
        put(field.at[FB, c, at], b, mask)
        put(field.at[FT, c, at], s, mask)
        if outs is not None and c < tiles - 1:
            spot = (pl.ds(pl.multiple_of(r - TOP, EDGE), EDGE), pl.ds(c * LANES, LANES))
            put(outs[2].at[spot], 0.5 * (a + b), mask)
            put(outs[3].at[spot], 0.5 * (a - b), mask)
            put(outs[4].at[spot], 0.5 * s, mask)


def motion(field, outs, r, mask, lane):
    tiles = field.shape[1]
    at = pl.ds(pl.multiple_of(r, EDGE), EDGE)
    dxa = along([field[FA, c, at, :] for c in range(tiles)], lane)
    dxt = along([field[FT, c, at, :] for c in range(tiles)], lane)
    for c in range(tiles):
        fx = dxa[c] + (read(field, FT, c, r, 1) - read(field, FT, c, r, -1))
        fy = dxt[c] + (read(field, FB, c, r, 1) - read(field, FB, c, r, -1))
        u = field[FU, c, at, :]
        v = field[FV, c, at, :]
        inertia = field[FM, c, at, :]
        ratio = field[FD, c, at, :]
        new_u = inertia * (u + 0.5 * v) + ratio * fx + field[FX, c, at, :]
        new_v = inertia * (v - 0.5 * u) + ratio * fy + field[FY, c, at, :]
        put(field.at[FU, c, at], new_u, mask)
        put(field.at[FV, c, at], new_v, mask)
        if outs is not None and c < tiles - 1:
            spot = (pl.ds(pl.multiple_of(r - TOP, EDGE), EDGE), pl.ds(c * LANES, LANES))
            put(outs[0].at[spot], new_u, mask)
            put(outs[1].at[spot], new_v, mask)


def sweep(field, outs, start, count, head, tail, skip=()):
    lane = lax.broadcasted_iota(jnp.int32, (EDGE, LANES), 1)
    line = lax.broadcasted_iota(jnp.int32, (EDGE, LANES), 0)

    def half(step, h, emit):
        for k in range(count):
            mask = None
            if k == 0 and head is not None:
                mask = line >= head(h)
            if k == count - 1 and tail is not None:
                mask = line < tail(h)
            step(field, outs if emit and k not in skip else None, start + EDGE * k, mask, lane)

    def cycle(t, carry):
        half(stress, 2 * t, False)
        half(motion, 2 * t + 1, False)
        return carry

    lax.fori_loop(0, SUB - 1, cycle, 0)
    half(stress, 2 * SUB - 2, True)
    half(motion, 2 * SUB - 1, True)


def kernel(
    lat_count,
    lon_count,
    weight,
    thick_hbm,
    area_hbm,
    top_hbm,
    land_hbm,
    u_hbm,
    v_hbm,
    s1_hbm,
    s2_hbm,
    s3_hbm,
    wx_hbm,
    wy_hbm,
    drag_hbm,
    field,
    out_u,
    out_v,
    out_1,
    out_2,
    out_3,
    own,
    other,
    thick,
    area,
    top,
    land,
    pack_left,
    pack_right,
    from_left,
    from_right,
    sum_left,
    sum_right,
    sum_from_left,
    sum_from_right,
    load_sem,
    field_sem,
    x_send,
    x_recv,
    halo_send,
    halo_recv,
):
    outs = (out_u, out_v, out_1, out_2, out_3)
    cats, rows, cols = thick.shape
    tiles = cols // LANES
    halo = tiles
    inner = tiles - 2
    last = cols - LANES
    pieces = rows // CHUNK
    events = (rows - 2 * EDGE - FINAL) // CHUNK
    my_cat = lax.axis_index("cat")
    my_lat = lax.axis_index("lat")
    my_lon = lax.axis_index("lon")
    partner = {"cat": 1 - my_cat}
    west = {"lon": lax.rem(my_lon + lon_count - 1, lon_count)}
    east = {"lon": lax.rem(my_lon + 1, lon_count)}
    north = {"lat": my_lat - 1}
    south = {"lat": my_lat + 1}
    has_north = my_lat > 0
    has_south = my_lat < lat_count - 1

    barrier = pltpu.get_barrier_semaphore()
    for device in (partner, west, east):
        pl.semaphore_signal(barrier, inc=1, device_id=device, device_id_type=MESH)

    @pl.when(has_north)
    def _():
        pl.semaphore_signal(barrier, inc=1, device_id=north, device_id_type=MESH)

    @pl.when(has_south)
    def _():
        pl.semaphore_signal(barrier, inc=1, device_id=south, device_id_type=MESH)

    groups = (
        (0, CHUNK, 0, LANES),
        (CHUNK, rows - CHUNK, 0, LANES),
        (0, rows, last, LANES),
        (0, rows, LANES, cols - 2 * LANES),
    )
    loads = []
    for k, (r0, height, c0, w) in enumerate(groups):
        spot = (pl.ds(r0, height), pl.ds(c0, w))
        group = (
            pltpu.make_async_copy(top_hbm.at[spot], top.at[spot], load_sem.at[3 * k]),
            pltpu.make_async_copy(
                thick_hbm.at[(slice(None),) + spot], thick.at[(slice(None),) + spot], load_sem.at[3 * k + 1]
            ),
            pltpu.make_async_copy(
                area_hbm.at[(slice(None),) + spot], area.at[(slice(None),) + spot], load_sem.at[3 * k + 2]
            ),
        )
        for copy in group:
            copy.start()
        loads.append(group)

    base = my_cat * cats

    def partial(r0, count, c0, w):
        def body(i, carry):
            r = pl.multiple_of(r0 + i * BLOCK, BLOCK)
            at = pl.ds(r, BLOCK)
            for c in range(c0, c0 + w):
                lanes = pl.ds(c * LANES, LANES)
                limit = top[at, lanes] - base
                strength = mass = conc = jnp.zeros((BLOCK, LANES), jnp.float32)
                for n in range(cats):
                    height = thick[n, at, lanes].astype(jnp.float32)
                    cover = jnp.where(limit > n, area[n, at, lanes].astype(jnp.float32), 0.0)
                    volume = cover * height
                    conc = conc + cover
                    mass = mass + volume
                    strength = strength + weight[n] * (volume * height)
                own[0, c, at, :] = strength
                own[1, c, at, :] = mass
                own[2, c, at, :] = conc
            return carry

        lax.fori_loop(0, count, body, 0)

    def exchange(slot, r0, height, c0, w):
        part = (pl.ds(0, 3), pl.ds(c0, w), pl.ds(r0, height))
        return pltpu.make_async_remote_copy(
            src_ref=own.at[part],
            dst_ref=other.at[part],
            send_sem=x_send.at[slot],
            recv_sem=x_recv.at[slot],
            device_id=partner,
            device_id_type=MESH,
        )

    def strip(i, c):
        return exchange((pieces if c else 0) + i, pl.multiple_of(i * CHUNK, CHUNK), CHUNK, c, 1)

    ends = (
        exchange(2 * pieces, 0, EDGE, 1, inner),
        exchange(2 * pieces + 1, rows - EDGE, EDGE, 1, inner),
    )
    final = exchange(2 * pieces + 2, rows - EDGE - FINAL, FINAL, 1, inner)

    def middle(e):
        return exchange(2 * pieces + 3 + e, pl.multiple_of(EDGE + e * CHUNK, EDGE), CHUNK, 1, inner)

    def total(r0, count, c0, w):
        for k in range(count):
            r = pl.multiple_of(r0 + k * EDGE, EDGE)
            at = pl.ds(r, EDGE)
            target = pl.ds(pl.multiple_of(r + TOP, EDGE), EDGE)
            for f in range(3):
                for c in range(c0, c0 + w):
                    field[f, c, target, :] = own[f, c, at, :] + other[f, c, at, :]

    for copy in loads[0]:
        copy.wait()
    partial(0, CHUNK // BLOCK, 0, 1)
    pl.semaphore_wait(barrier, 3 + has_north.astype(jnp.int32) + has_south.astype(jnp.int32))
    strip(0, 0).start()

    def send_strip(c):
        def body(i, carry):
            partial(i * CHUNK, CHUNK // BLOCK, c, 1)
            strip(i, c).start()
            return carry

        return body

    for copy in loads[1]:
        copy.wait()
    lax.fori_loop(1, pieces, send_strip(0), 0)

    land_load = pltpu.make_async_copy(land_hbm, land, load_sem.at[12])
    land_load.start()
    field_loads = []
    for k, (f, ref) in enumerate(
        (
            (FU, u_hbm),
            (FV, v_hbm),
            (FA, s1_hbm),
            (FB, s2_hbm),
            (FT, s3_hbm),
            (FX, wx_hbm),
            (FY, wy_hbm),
            (FD, drag_hbm),
        )
    ):
        for c in range(tiles):
            copy = pltpu.make_async_copy(
                ref.at[:, pl.ds(c * LANES, LANES)],
                field.at[f, c, pl.ds(TOP, rows)],
                field_sem.at[k * tiles + c],
            )
            copy.start()
            field_loads.append(copy)

    @pl.when(jnp.logical_not(has_north))
    def _():
        field[:, :, pl.ds(TOP - EDGE, EDGE), :] = jnp.zeros((FIELDS, tiles + 1, EDGE, LANES), jnp.float32)

    @pl.when(jnp.logical_not(has_south))
    def _():
        field[:, :, pl.ds(TOP + rows, EDGE), :] = jnp.zeros((FIELDS, tiles + 1, EDGE, LANES), jnp.float32)

    for copy in loads[2]:
        copy.wait()
    lax.fori_loop(0, pieces, send_strip(tiles - 1), 0)
    for copy in loads[3]:
        copy.wait()
    partial(0, 1, 1, inner)
    ends[0].start()
    partial(rows - BLOCK, 1, 1, inner)
    ends[1].start()

    def send_middle(e, carry):
        partial(BLOCK + e * CHUNK, CHUNK // BLOCK, 1, inner)
        middle(e).start()
        return carry

    lax.fori_loop(0, events, send_middle, 0)
    final.start()

    land_load.wait()

    def wet_body(i, carry):
        r = pl.multiple_of(i * BLOCK, BLOCK)
        for c in range(tiles):
            field[FW, c, pl.ds(pl.multiple_of(r + TOP, EDGE), BLOCK), :] = land[
                pl.ds(r, BLOCK), pl.ds(c * LANES, LANES)
            ].astype(jnp.float32)
        return carry

    lax.fori_loop(0, rows // BLOCK, wet_body, 0)
    for copy in field_loads:
        copy.wait()

    def lon_start(entries, buffers, slot):
        left_out, right_out, left_in, right_in = buffers

        def body(i, carry):
            r = pl.multiple_of(i * CHUNK, 8)
            lane = lax.broadcasted_iota(jnp.int32, (CHUNK, LANES), 1)
            left = right = None
            for k, (f, offset) in enumerate(entries):
                source = pl.ds(pl.multiple_of(r + (TOP + offset), 8), CHUNK)
                x = field[f, 0, source, :]
                y = field[f, tiles - 1, source, :]
                if k == 0:
                    left, right = x, y
                else:
                    shift = EDGE * k
                    left = jnp.where(lane >= shift, pltpu.roll(x, shift, 1), left)
                    right = jnp.where(lane < LANES - shift, pltpu.roll(y, LANES - shift, 1), right)
            left_out[pl.ds(r, CHUNK), :] = left
            right_out[pl.ds(r, CHUNK), :] = right
            return carry

        lax.fori_loop(0, left_out.shape[0] // CHUNK, body, 0)
        copies = tuple(
            pltpu.make_async_remote_copy(
                src_ref=source,
                dst_ref=target,
                send_sem=halo_send.at[slot + k],
                recv_sem=halo_recv.at[slot + k],
                device_id=device,
                device_id_type=MESH,
            )
            for k, (source, target, device) in enumerate(
                ((right_out, left_in, east), (left_out, right_in, west))
            )
        )
        for copy in copies:
            copy.start()
        return copies

    def lon_finish(entries, buffers, copies):
        left_in, right_in = buffers[2:]
        for copy in copies:
            copy.wait()

        def body(i, carry):
            r = pl.multiple_of(i * CHUNK, 8)
            lane = lax.broadcasted_iota(jnp.int32, (CHUNK, LANES), 1)
            x = right_in[pl.ds(r, CHUNK), :]
            y = left_in[pl.ds(r, CHUNK), :]
            for k, (f, offset) in enumerate(entries):
                a = pltpu.roll(x, LANES - EDGE * k, 1) if k else x
                b = pltpu.roll(y, EDGE * k, 1) if k else y
                target = pl.ds(pl.multiple_of(r + (TOP + offset), 8), CHUNK)
                field[f, halo, target, :] = jnp.where(
                    lane < EDGE, a, jnp.where(lane >= LANES - EDGE, b, 0.0)
                )
            return carry

        lax.fori_loop(0, left_in.shape[0] // CHUNK, body, 0)

    def lat_start(first, count, slot):
        def row_copy(source, target, at, device):
            return pltpu.make_async_remote_copy(
                src_ref=field.at[pl.ds(first, count), :, pl.ds(source, EDGE), :],
                dst_ref=field.at[pl.ds(first, count), :, pl.ds(target, EDGE), :],
                send_sem=halo_send.at[at],
                recv_sem=halo_recv.at[at],
                device_id=device,
                device_id_type=MESH,
            )

        to_north = row_copy(TOP, TOP + rows, slot, north)
        to_south = row_copy(TOP + rows - EDGE, TOP - EDGE, slot + 1, south)

        @pl.when(has_north)
        def _():
            to_north.start()

        @pl.when(has_south)
        def _():
            to_south.start()

        return to_north, to_south

    def lat_finish(to_north, to_south):
        @pl.when(has_north)
        def _():
            to_north.wait_send()
            to_south.wait_recv()

        @pl.when(has_south)
        def _():
            to_south.wait_send()
            to_north.wait_recv()

    wide_pack = (pack_left, pack_right, from_left, from_right)
    input_entries = [(f, 0) for f in range(3, FIELDS)]
    input_copies = lon_start(input_entries, wide_pack, 0)
    lon_finish(input_entries, wide_pack, input_copies)
    input_rows = lat_start(3, FIELDS - 3, 2)

    def sum_strip(c):
        def body(i, carry):
            strip(i, c).wait()
            total(i * CHUNK, CHUNK // EDGE, c, 1)
            return carry

        return body

    lax.fori_loop(0, pieces, sum_strip(0), 0)
    lax.fori_loop(0, pieces, sum_strip(tiles - 1), 0)
    for copy, r0 in zip(ends, (0, rows - EDGE)):
        copy.wait()
        total(r0, 1, 1, inner)
    short = rows // FOLD
    sum_pack = (sum_left, sum_right, sum_from_left, sum_from_right)
    sum_entries = [(f, g * short) for g in range(FOLD) for f in range(3)]
    sum_copies = lon_start(sum_entries, sum_pack, 4)
    lon_finish(sum_entries, sum_pack, sum_copies)
    sum_rows = lat_start(0, 3, 6)
    lat_finish(*input_rows)
    lat_finish(*sum_rows)

    bottom = TOP + rows - EDGE
    for k in range(2):
        derive(field, bottom + EDGE * k)
    sweep(field, outs, bottom, 2, lambda h: h, None, skip=(1,))

    middle(0).wait()
    total(EDGE, CHUNK // EDGE, 1, inner)
    count = CHUNK // EDGE + 2
    for k in range(count):
        derive(field, TOP - EDGE + EDGE * k)
    sweep(field, outs, TOP - EDGE, count, None, lambda h: EDGE - h, skip=(0,))

    def event(e, carry):
        middle(e).wait()
        r = EDGE + e * CHUNK
        total(r, CHUNK // EDGE, 1, inner)
        for k in range(CHUNK // EDGE):
            derive(field, TOP + r + EDGE * k)
        sweep(
            field,
            outs,
            TOP + r - EDGE,
            CHUNK // EDGE + 1,
            lambda h: EDGE - h,
            lambda h: EDGE - h,
        )
        return carry

    lax.fori_loop(1, events, event, 0)
    final.wait()
    total(rows - EDGE - FINAL, FINAL // EDGE, 1, inner)


def finish(*refs):
    sem = refs[-1]
    results = refs[6:11]
    field = refs[11]
    outs = refs[12:17]
    rows = outs[0].shape[0]
    cone = FINAL + 2 * EDGE
    done = rows - cone

    def write(k, r0, height, slot):
        at = pl.ds(r0, height)
        return pltpu.make_async_copy(outs[k].at[at], results[k].at[at], sem.at[slot])

    early = [write(k, 0, done, k) for k in range(5)]
    for copy in early:
        copy.start()
    start = TOP + done
    for k in range(FINAL // EDGE):
        derive(field, start + EDGE + EDGE * k)
    sweep(field, outs, start, cone // EDGE, lambda h: EDGE - h, lambda h: h)
    late = [write(k, done, cone, 5 + k) for k in range(5)]
    for copy in late:
        copy.start()
    for copy in early + late:
        copy.wait()


def shards(
    lat_count,
    lon_count,
    thickness,
    area,
    ridge_weight,
    cat_top,
    land_mask,
    velocity_u,
    velocity_v,
    stress_div,
    stress_ten,
    stress_shear,
    wind_x,
    wind_y,
    water_drag,
):
    cats, rows, cols = thickness.shape
    tiles = cols // LANES
    tall = rows + 2 * TOP
    f32 = jnp.float32
    events = (rows - 2 * EDGE - FINAL) // CHUNK
    pieces = rows // CHUNK
    slots = 2 * pieces + 3 + events
    anywhere = pl.BlockSpec(memory_space=pl.ANY)
    vmem = pl.BlockSpec(memory_space=pltpu.VMEM)
    state = (pltpu.VMEM((FIELDS, tiles + 1, tall, LANES), f32),) + tuple(
        pltpu.VMEM((rows, cols), f32) for _ in range(5)
    )
    results = pl.pallas_call(
        functools.partial(kernel, lat_count, lon_count),
        out_shape=state,
        in_specs=[pl.BlockSpec(memory_space=pltpu.SMEM)] + [anywhere] * 12,
        out_specs=(vmem,) * 6,
        scratch_shapes=[
            pltpu.VMEM((3, tiles, rows, LANES), f32),
            pltpu.VMEM((3, tiles, rows, LANES), f32),
            pltpu.VMEM((cats, rows, cols), thickness.dtype),
            pltpu.VMEM((cats, rows, cols), area.dtype),
            pltpu.VMEM((rows, cols), jnp.int32),
            pltpu.VMEM((rows, cols), jnp.int32),
            pltpu.VMEM((rows, LANES), f32),
            pltpu.VMEM((rows, LANES), f32),
            pltpu.VMEM((rows, LANES), f32),
            pltpu.VMEM((rows, LANES), f32),
            pltpu.VMEM((rows // FOLD, LANES), f32),
            pltpu.VMEM((rows // FOLD, LANES), f32),
            pltpu.VMEM((rows // FOLD, LANES), f32),
            pltpu.VMEM((rows // FOLD, LANES), f32),
            pltpu.SemaphoreType.DMA((13,)),
            pltpu.SemaphoreType.DMA((8 * tiles,)),
            pltpu.SemaphoreType.DMA((slots,)),
            pltpu.SemaphoreType.DMA((slots,)),
            pltpu.SemaphoreType.DMA((8,)),
            pltpu.SemaphoreType.DMA((8,)),
        ],
        compiler_params=pltpu.CompilerParams(
            collective_id=0, has_side_effects=True, vmem_limit_bytes=44 * 2**20
        ),
        name="ice",
    )(
        ridge_weight,
        thickness,
        area,
        cat_top,
        land_mask,
        velocity_u,
        velocity_v,
        stress_div,
        stress_ten,
        stress_shear,
        wind_x,
        wind_y,
        water_drag,
    )
    return pl.pallas_call(
        finish,
        out_shape=tuple(jax.ShapeDtypeStruct((rows, cols), f32) for _ in range(5)) + state,
        in_specs=[vmem] * 6,
        out_specs=(anywhere,) * 5 + (vmem,) * 6,
        input_output_aliases={k: 5 + k for k in range(6)},
        scratch_shapes=[pltpu.SemaphoreType.DMA((10,))],
        compiler_params=pltpu.CompilerParams(vmem_limit_bytes=4 * 2**20),
        name="finish",
    )(*results)[:5]


def solution(mesh):
    body = functools.partial(shards, mesh.shape["lat"], mesh.shape["lon"])
    plane = P("lat", "lon")
    return jax.shard_map(
        body,
        mesh=mesh,
        in_specs=(P("cat", "lat", "lon"), P("cat", "lat", "lon"), P("cat")) + (plane,) * 10,
        out_specs=(plane,) * 5,
        check_vma=False,
    )
```

profile of v0, /device:TPU:0, one launch (start us, length us, event | category | flops | bytes accessed | tf_op | source)
XLA Modules:
  0.0 54.6 jit_solution(5968242224735666764)
XLA Ops:
  0.6 51.8 %ice.1 = (f32[12,6,288,128]{3,2,1,0:T(8,128)S(1)}, f32[256,640]{1,0:T(8,128)S(1)}, f32[256,640]{1,0:T(8,128)S(1)}, f32[256,640]{1,0:T(8,128)S(1)}, f32[256,640]{1,0:T(8,128)S(1)}, /*index=5*/f32[256,640]{1,0:T(8,128)S(1)}) custom-call(f32[20]{0:T(128)} %weight.1, bf16[20,256,640]{2,1,0:T(8,128)(2,1)} %thick_hbm.1, bf16[20,256,640]{2,1,0:T(8,128)(2,1)} %area_hbm.1, ...), custom_call_target="tpu_custom_call" | custom-call | tf_op jit(solution)/shard_map/ice/pallas_call | solution.py:592
  52.4 2.2 %finish.1 = (f32[256,640]{1,0:T(8,128)}, f32[256,640]{1,0:T(8,128)}, f32[256,640]{1,0:T(8,128)}, f32[256,640]{1,0:T(8,128)}, f32[256,640]{1,0:T(8,128)}, /*index...) custom-call(f32[12,6,288,128]{3,2,1,0:T(8,128)S(1)} %get-tuple-eleme, ...), custom_call_target="tpu_custom_call", output_to_operand_aliasing={{5}: (0, {}), {6}: (1, {}), {7}: (2, {}), {8}: (3, {}), {9}... | custom-call | tf_op jit(solution)/shard_map/finish/pallas_call | solution.py:638
where the time goes:
time: 54.8 us; the launch traced here: 54.6 us
  Pallas kernels  54 us (99%)
  between operations  0.64 us (1%)
    pallas_call x1, Pallas kernels, shards(): pl.pallas_call(functools.partial(kernel, lat_count, lon_count), out_shape...  51.8 us
    pallas_call x1, Pallas kernels, shards(): pl.pallas_call(finish, out_shape=tuple((jax.ShapeDtypeStruct((rows, cols)...  2.21 us

commit v1 on v0

--- a/solution.py
+++ b/solution.py
@@ -12,6 +12,7 @@
 EDGE = 8
 BLOCK = 16
 CHUNK = 32
+TAIL = (16, 16)
 FINAL = 16
 TOP = 16
 FOLD = 4
@@ -120,7 +121,7 @@
             put(outs[1].at[spot], new_v, mask)
 
 
-def sweep(field, outs, start, count, head, tail, skip=()):
+def sweep(field, outs, start, count, head, tail, skip=(), between=None):
     lane = lax.broadcasted_iota(jnp.int32, (EDGE, LANES), 1)
     line = lax.broadcasted_iota(jnp.int32, (EDGE, LANES), 0)
 
@@ -140,13 +141,15 @@
 
     lax.fori_loop(0, SUB - 1, cycle, 0)
     half(stress, 2 * SUB - 2, True)
+    if between is not None:
+        between()
     half(motion, 2 * SUB - 1, True)
 
 
 def kernel(
     lat_count,
     lon_count,
-    weight,
+    weight_hbm,
     thick_hbm,
     area_hbm,
     top_hbm,
@@ -165,6 +168,7 @@
     out_1,
     out_2,
     out_3,
+    weight,
     own,
     other,
     thick,
@@ -185,6 +189,7 @@
     x_recv,
     halo_send,
     halo_recv,
+    ready,
 ):
     outs = (out_u, out_v, out_1, out_2, out_3)
     cats, rows, cols = thick.shape
@@ -193,7 +198,7 @@
     inner = tiles - 2
     last = cols - LANES
     pieces = rows // CHUNK
-    events = (rows - 2 * EDGE - FINAL) // CHUNK
+    events = (rows - 2 * EDGE - FINAL - sum(TAIL)) // CHUNK
     my_cat = lax.axis_index("cat")
     my_lat = lax.axis_index("lat")
     my_lon = lax.axis_index("lon")
@@ -205,17 +210,22 @@
     has_north = my_lat > 0
     has_south = my_lat < lat_count - 1
 
+    early = lax.rem(my_lat + my_lon, 2) == 0
+    late = jnp.logical_not(early)
+    around = 2 + has_north.astype(jnp.int32) + has_south.astype(jnp.int32)
     barrier = pltpu.get_barrier_semaphore()
-    for device in (partner, west, east):
-        pl.semaphore_signal(barrier, inc=1, device_id=device, device_id_type=MESH)
-
-    @pl.when(has_north)
-    def _():
-        pl.semaphore_signal(barrier, inc=1, device_id=north, device_id_type=MESH)
-
-    @pl.when(has_south)
-    def _():
-        pl.semaphore_signal(barrier, inc=1, device_id=south, device_id_type=MESH)
+    pl.semaphore_signal(barrier, inc=1, device_id=partner, device_id_type=MESH)
+
+    def greet(semaphore, when):
+        for device, there in ((west, when), (east, when), (north, when & has_north), (south, when & has_south)):
+
+            @pl.when(there)
+            def _():
+                pl.semaphore_signal(semaphore, inc=1, device_id=device, device_id_type=MESH)
+
+    greet(barrier, early)
+    weight_load = pltpu.make_async_copy(weight_hbm, weight, load_sem.at[13])
+    weight_load.start()
 
     groups = (
         (0, CHUNK, 0, LANES),
@@ -286,6 +296,12 @@
     def middle(e):
         return exchange(2 * pieces + 3 + e, pl.multiple_of(EDGE + e * CHUNK, EDGE), CHUNK, 1, inner)
 
+    tail_rows = [EDGE + events * CHUNK + sum(TAIL[:k]) for k in range(len(TAIL))]
+    tail = [
+        exchange(2 * pieces + 3 + events + k, r0, height, 1, inner)
+        for k, (r0, height) in enumerate(zip(tail_rows, TAIL))
+    ]
+
     def total(r0, count, c0, w):
         for k in range(count):
             r = pl.multiple_of(r0 + k * EDGE, EDGE)
@@ -295,11 +311,13 @@
                 for c in range(c0, c0 + w):
                     field[f, c, target, :] = own[f, c, at, :] + other[f, c, at, :]
 
+    weight_load.wait()
     for copy in loads[0]:
         copy.wait()
     partial(0, CHUNK // BLOCK, 0, 1)
-    pl.semaphore_wait(barrier, 3 + has_north.astype(jnp.int32) + has_south.astype(jnp.int32))
+    pl.semaphore_wait(barrier, jnp.where(early, 1, 1 + around))
     strip(0, 0).start()
+    greet(ready, late)
 
     def send_strip(c):
         def body(i, carry):
@@ -361,6 +379,10 @@
         return carry
 
     lax.fori_loop(0, events, send_middle, 0)
+    reached = BLOCK + events * CHUNK
+    partial(reached, (rows - BLOCK - reached) // BLOCK, 1, inner)
+    for copy in tail:
+        copy.start()
     final.start()
 
     land_load.wait()
@@ -474,6 +496,11 @@
 
     wide_pack = (pack_left, pack_right, from_left, from_right)
     input_entries = [(f, 0) for f in range(3, FIELDS)]
+
+    @pl.when(early)
+    def _():
+        pl.semaphore_wait(ready, around)
+
     input_copies = lon_start(input_entries, wide_pack, 0)
     lon_finish(input_entries, wide_pack, input_copies)
     input_rows = lat_start(3, FIELDS - 3, 2)
@@ -512,23 +539,28 @@
         derive(field, TOP - EDGE + EDGE * k)
     sweep(field, outs, TOP - EDGE, count, None, lambda h: EDGE - h, skip=(0,))
 
-    def event(e, carry):
-        middle(e).wait()
-        r = EDGE + e * CHUNK
-        total(r, CHUNK // EDGE, 1, inner)
-        for k in range(CHUNK // EDGE):
+    def advance(r, height):
+        total(r, height // EDGE, 1, inner)
+        for k in range(height // EDGE):
             derive(field, TOP + r + EDGE * k)
         sweep(
             field,
             outs,
             TOP + r - EDGE,
-            CHUNK // EDGE + 1,
+            height // EDGE + 1,
             lambda h: EDGE - h,
             lambda h: EDGE - h,
         )
+
+    def event(e, carry):
+        middle(e).wait()
+        advance(EDGE + e * CHUNK, CHUNK)
         return carry
 
     lax.fori_loop(1, events, event, 0)
+    for copy, r0, height in zip(tail, tail_rows, TAIL):
+        copy.wait()
+        advance(r0, height)
     final.wait()
     total(rows - EDGE - FINAL, FINAL // EDGE, 1, inner)
 
@@ -552,9 +584,14 @@
     start = TOP + done
     for k in range(FINAL // EDGE):
         derive(field, start + EDGE + EDGE * k)
-    sweep(field, outs, start, cone // EDGE, lambda h: EDGE - h, lambda h: h)
     late = [write(k, done, cone, 5 + k) for k in range(5)]
-    for copy in late:
+
+    def write_stress():
+        for copy in late[2:]:
+            copy.start()
+
+    sweep(field, outs, start, cone // EDGE, lambda h: EDGE - h, lambda h: h, between=write_stress)
+    for copy in late[:2]:
         copy.start()
     for copy in early + late:
         copy.wait()
@@ -581,9 +618,9 @@
     tiles = cols // LANES
     tall = rows + 2 * TOP
     f32 = jnp.float32
-    events = (rows - 2 * EDGE - FINAL) // CHUNK
+    events = (rows - 2 * EDGE - FINAL - sum(TAIL)) // CHUNK
     pieces = rows // CHUNK
-    slots = 2 * pieces + 3 + events
+    slots = 2 * pieces + 3 + events + len(TAIL)
     anywhere = pl.BlockSpec(memory_space=pl.ANY)
     vmem = pl.BlockSpec(memory_space=pltpu.VMEM)
     state = (pltpu.VMEM((FIELDS, tiles + 1, tall, LANES), f32),) + tuple(
@@ -592,9 +629,10 @@
     results = pl.pallas_call(
         functools.partial(kernel, lat_count, lon_count),
         out_shape=state,
-        in_specs=[pl.BlockSpec(memory_space=pltpu.SMEM)] + [anywhere] * 12,
+        in_specs=[anywhere] * 13,
         out_specs=(vmem,) * 6,
         scratch_shapes=[
+            pltpu.SMEM((cats,), f32),
             pltpu.VMEM((3, tiles, rows, LANES), f32),
             pltpu.VMEM((3, tiles, rows, LANES), f32),
             pltpu.VMEM((cats, rows, cols), thickness.dtype),
@@ -609,12 +647,13 @@
             pltpu.VMEM((rows // FOLD, LANES), f32),
             pltpu.VMEM((rows // FOLD, LANES), f32),
             pltpu.VMEM((rows // FOLD, LANES), f32),
-            pltpu.SemaphoreType.DMA((13,)),
+            pltpu.SemaphoreType.DMA((14,)),
             pltpu.SemaphoreType.DMA((8 * tiles,)),
             pltpu.SemaphoreType.DMA((slots,)),
             pltpu.SemaphoreType.DMA((slots,)),
             pltpu.SemaphoreType.DMA((8,)),
             pltpu.SemaphoreType.DMA((8,)),
+            pltpu.SemaphoreType.REGULAR,
         ],
         compiler_params=pltpu.CompilerParams(
             collective_id=0, has_side_effects=True, vmem_limit_bytes=44 * 2**20

time: 54.8 us -> 52.3 us (0.954)
  the two profiles are of different devices: /device:TPU:0 before, /device:TPU:1 now
where the time goes in v1:
time: 52.3 us; the launch traced here: 52.1 us
  Pallas kernels  51.4 us (98%)
  between operations  0.64 us (1%)
    pallas_call x1, Pallas kernels, shards(): pl.pallas_call(functools.partial(kernel, lat_count, lon_count), out_shape...  49.3 us
    pallas_call x1, Pallas kernels, shards(): pl.pallas_call(finish, out_shape=tuple((jax.ShapeDtypeStruct((rows, cols)...  2.13 us

profile of v1, /device:TPU:1, one launch (start us, length us, event | category | flops | bytes accessed | tf_op | source)
XLA Modules:
  0.0 52.1 jit_solution(7144283824814074732)
XLA Ops:
  0.6 49.3 %ice.1 = (f32[12,6,288,128]{3,2,1,0:T(8,128)S(1)}, f32[256,640]{1,0:T(8,128)S(1)}, f32[256,640]{1,0:T(8,128)S(1)}, f32[256,640]{1,0:T(8,128)S(1)}, f32[256,640]{1,0:T(8,128)S(1)}, /*index=5*/f32[256,640]{1,0:T(8,128)S(1)}) custom-call(f32[20]{0:T(128)} %weight_hbm.1, bf16[20,256,640]{2,1,0:T(8,128)(2,1)} %thick_hbm.1, bf16[20,256,640]{2,1,0:T(8,128)(2,1)} %area_hbm.1, ...), custom_call_target="tpu_custom_call" | custom-call | tf_op jit(solution)/shard_map/ice/pallas_call | solution.py:629
  50.0 2.1 %finish.1 = (f32[256,640]{1,0:T(8,128)}, f32[256,640]{1,0:T(8,128)}, f32[256,640]{1,0:T(8,128)}, f32[256,640]{1,0:T(8,128)}, f32[256,640]{1,0:T(8,128)}, /*index...) custom-call(f32[12,6,288,128]{3,2,1,0:T(8,128)S(1)} %get-tuple-eleme, ...), custom_call_target="tpu_custom_call", output_to_operand_aliasing={{5}: (0, {}), {6}: (1, {}), {7}: (2, {}), {8}: (3, {}), {9}... | custom-call | tf_op jit(solution)/shard_map/finish/pallas_call | solution.py:677

commit v2 on v1

--- a/solution.py
+++ b/solution.py
@@ -15,6 +15,9 @@
 TAIL = (16, 16)
 FINAL = 16
 TOP = 16
+LEFT = (16, 48, 64, 128)
+RIGHT = (128, 128)
+PAIR = 1
 FOLD = 4
 MESH = pl.DeviceIdType.MESH
 
@@ -121,7 +124,7 @@
             put(outs[1].at[spot], new_v, mask)
 
 
-def sweep(field, outs, start, count, head, tail, skip=(), between=None):
+def sweep(field, outs, start, count, head, tail, skip=(), between=None, unroll=False):
     lane = lax.broadcasted_iota(jnp.int32, (EDGE, LANES), 1)
     line = lax.broadcasted_iota(jnp.int32, (EDGE, LANES), 0)
 
@@ -139,7 +142,11 @@
         half(motion, 2 * t + 1, False)
         return carry
 
-    lax.fori_loop(0, SUB - 1, cycle, 0)
+    if unroll:
+        for t in range(SUB - 1):
+            cycle(t, 0)
+    else:
+        lax.fori_loop(0, SUB - 1, cycle, 0)
     half(stress, 2 * SUB - 2, True)
     if between is not None:
         between()
@@ -190,6 +197,7 @@
     halo_send,
     halo_recv,
     ready,
+    token,
 ):
     outs = (out_u, out_v, out_1, out_2, out_3)
     cats, rows, cols = thick.shape
@@ -197,7 +205,6 @@
     halo = tiles
     inner = tiles - 2
     last = cols - LANES
-    pieces = rows // CHUNK
     events = (rows - 2 * EDGE - FINAL - sum(TAIL)) // CHUNK
     my_cat = lax.axis_index("cat")
     my_lat = lax.axis_index("lat")
@@ -210,26 +217,11 @@
     has_north = my_lat > 0
     has_south = my_lat < lat_count - 1
 
-    early = lax.rem(my_lat + my_lon, 2) == 0
-    late = jnp.logical_not(early)
-    around = 2 + has_north.astype(jnp.int32) + has_south.astype(jnp.int32)
-    barrier = pltpu.get_barrier_semaphore()
-    pl.semaphore_signal(barrier, inc=1, device_id=partner, device_id_type=MESH)
-
-    def greet(semaphore, when):
-        for device, there in ((west, when), (east, when), (north, when & has_north), (south, when & has_south)):
-
-            @pl.when(there)
-            def _():
-                pl.semaphore_signal(semaphore, inc=1, device_id=device, device_id_type=MESH)
-
-    greet(barrier, early)
-    weight_load = pltpu.make_async_copy(weight_hbm, weight, load_sem.at[13])
-    weight_load.start()
 
     groups = (
-        (0, CHUNK, 0, LANES),
-        (CHUNK, rows - CHUNK, 0, LANES),
+        (0, LEFT[0], 0, LANES),
+        (LEFT[0], LEFT[1], 0, LANES),
+        (LEFT[0] + LEFT[1], rows - LEFT[0] - LEFT[1], 0, LANES),
         (0, rows, last, LANES),
         (0, rows, LANES, cols - 2 * LANES),
     )
@@ -245,10 +237,37 @@
                 area_hbm.at[(slice(None),) + spot], area.at[(slice(None),) + spot], load_sem.at[3 * k + 2]
             ),
         )
-        for copy in group:
-            copy.start()
         loads.append(group)
 
+    def load(*which):
+        for k in which:
+            for copy in loads[k]:
+                copy.start()
+
+    def loaded(k):
+        for copy in loads[k]:
+            copy.wait()
+
+    load(0)
+    weight_load = pltpu.make_async_copy(weight_hbm, weight, load_sem.at[16])
+    weight_load.start()
+    load(1)
+
+    has_west = my_lon > 0
+    has_east = my_lon < lon_count - 1
+    before = 1 + has_north.astype(jnp.int32) + has_west.astype(jnp.int32)
+    after = has_south.astype(jnp.int32) + has_east.astype(jnp.int32)
+    barrier = pltpu.get_barrier_semaphore()
+    pl.semaphore_signal(barrier, inc=1, device_id=partner, device_id_type=MESH)
+
+    def greet(semaphore, *devices):
+        for device, there in devices:
+
+            @pl.when(there)
+            def _():
+                pl.semaphore_signal(semaphore, inc=1, device_id=device, device_id_type=MESH)
+
+    greet(barrier, (south, has_south), (east, has_east))
     base = my_cat * cats
 
     def partial(r0, count, c0, w):
@@ -284,21 +303,33 @@
             device_id_type=MESH,
         )
 
-    def strip(i, c):
-        return exchange((pieces if c else 0) + i, pl.multiple_of(i * CHUNK, CHUNK), CHUNK, c, 1)
+    strips = []
+    for c, heights in ((0, LEFT), (tiles - 1, RIGHT)):
+        for k, height in enumerate(heights):
+            strips.append((sum(heights[:k]), height, c))
+
+    def strip(k):
+        r0, height, c = strips[k]
+        return exchange(k, r0, height, c, 1)
+
+    def send_strip(k):
+        r0, height, c = strips[k]
+        partial(r0, height // BLOCK, c, 1)
+        strip(k).start()
 
     ends = (
-        exchange(2 * pieces, 0, EDGE, 1, inner),
-        exchange(2 * pieces + 1, rows - EDGE, EDGE, 1, inner),
+        exchange(len(strips), 0, EDGE, 1, inner),
+        exchange(len(strips) + 1, rows - EDGE, EDGE, 1, inner),
     )
-    final = exchange(2 * pieces + 2, rows - EDGE - FINAL, FINAL, 1, inner)
+    final = exchange(len(strips) + 2, rows - EDGE - FINAL, FINAL, 1, inner)
 
     def middle(e):
-        return exchange(2 * pieces + 3 + e, pl.multiple_of(EDGE + e * CHUNK, EDGE), CHUNK, 1, inner)
+        r = pl.multiple_of(EDGE + e * (PAIR * CHUNK), EDGE)
+        return exchange(len(strips) + 3 + e, r, PAIR * CHUNK, 1, inner)
 
     tail_rows = [EDGE + events * CHUNK + sum(TAIL[:k]) for k in range(len(TAIL))]
     tail = [
-        exchange(2 * pieces + 3 + events + k, r0, height, 1, inner)
+        exchange(len(strips) + 3 + events // PAIR + k, r0, height, 1, inner)
         for k, (r0, height) in enumerate(zip(tail_rows, TAIL))
     ]
 
@@ -312,26 +343,20 @@
                     field[f, c, target, :] = own[f, c, at, :] + other[f, c, at, :]
 
     weight_load.wait()
-    for copy in loads[0]:
-        copy.wait()
-    partial(0, CHUNK // BLOCK, 0, 1)
-    pl.semaphore_wait(barrier, jnp.where(early, 1, 1 + around))
-    strip(0, 0).start()
-    greet(ready, late)
-
-    def send_strip(c):
-        def body(i, carry):
-            partial(i * CHUNK, CHUNK // BLOCK, c, 1)
-            strip(i, c).start()
-            return carry
-
-        return body
-
-    for copy in loads[1]:
-        copy.wait()
-    lax.fori_loop(1, pieces, send_strip(0), 0)
-
-    land_load = pltpu.make_async_copy(land_hbm, land, load_sem.at[12])
+    loaded(0)
+    load(2)
+    partial(0, LEFT[0] // BLOCK, 0, 1)
+    pl.semaphore_wait(barrier, before)
+    strip(0).start()
+    load(3, 4)
+    greet(ready, (north, has_north), (west, has_west))
+    loaded(1)
+    send_strip(1)
+    loaded(2)
+    for k in range(2, len(LEFT)):
+        send_strip(k)
+
+    land_load = pltpu.make_async_copy(land_hbm, land, load_sem.at[15])
     land_load.start()
     field_loads = []
     for k, (f, ref) in enumerate(
@@ -363,22 +388,21 @@
     def _():
         field[:, :, pl.ds(TOP + rows, EDGE), :] = jnp.zeros((FIELDS, tiles + 1, EDGE, LANES), jnp.float32)
 
-    for copy in loads[2]:
-        copy.wait()
-    lax.fori_loop(0, pieces, send_strip(tiles - 1), 0)
-    for copy in loads[3]:
-        copy.wait()
+    loaded(3)
+    for k in range(len(LEFT), len(strips)):
+        send_strip(k)
+    loaded(4)
     partial(0, 1, 1, inner)
     ends[0].start()
     partial(rows - BLOCK, 1, 1, inner)
     ends[1].start()
 
     def send_middle(e, carry):
-        partial(BLOCK + e * CHUNK, CHUNK // BLOCK, 1, inner)
+        partial(BLOCK + e * (PAIR * CHUNK), PAIR * CHUNK // BLOCK, 1, inner)
         middle(e).start()
         return carry
 
-    lax.fori_loop(0, events, send_middle, 0)
+    lax.fori_loop(0, events // PAIR, send_middle, 0)
     reached = BLOCK + events * CHUNK
     partial(reached, (rows - BLOCK - reached) // BLOCK, 1, inner)
     for copy in tail:
@@ -497,24 +521,35 @@
     wide_pack = (pack_left, pack_right, from_left, from_right)
     input_entries = [(f, 0) for f in range(3, FIELDS)]
 
-    @pl.when(early)
+    @pl.when(after > 0)
     def _():
-        pl.semaphore_wait(ready, around)
+        pl.semaphore_wait(ready, after)
+
+    @pl.when(has_west)
+    def _():
+        pl.semaphore_wait(token.at[0], 1)
+
+    @pl.when(has_east)
+    def _():
+        pl.semaphore_signal(token.at[0], inc=1, device_id=east, device_id_type=MESH)
+        pl.semaphore_wait(token.at[1], 1)
+
+    @pl.when(has_west)
+    def _():
+        pl.semaphore_signal(token.at[1], inc=1, device_id=west, device_id_type=MESH)
 
     input_copies = lon_start(input_entries, wide_pack, 0)
     lon_finish(input_entries, wide_pack, input_copies)
     input_rows = lat_start(3, FIELDS - 3, 2)
 
-    def sum_strip(c):
-        def body(i, carry):
-            strip(i, c).wait()
-            total(i * CHUNK, CHUNK // EDGE, c, 1)
+    for k, (r0, height, c) in enumerate(strips):
+        strip(k).wait()
+
+        def sum_body(i, carry):
+            total(r0 + i * BLOCK, BLOCK // EDGE, c, 1)
             return carry
 
-        return body
-
-    lax.fori_loop(0, pieces, sum_strip(0), 0)
-    lax.fori_loop(0, pieces, sum_strip(tiles - 1), 0)
+        lax.fori_loop(0, height // BLOCK, sum_body, 0)
     for copy, r0 in zip(ends, (0, rows - EDGE)):
         copy.wait()
         total(r0, 1, 1, inner)
@@ -553,7 +588,10 @@
         )
 
     def event(e, carry):
-        middle(e).wait()
+        @pl.when(lax.rem(e, PAIR) == 0)
+        def _():
+            middle(e // PAIR).wait()
+
         advance(EDGE + e * CHUNK, CHUNK)
         return carry
 
@@ -590,7 +628,7 @@
         for copy in late[2:]:
             copy.start()
 
-    sweep(field, outs, start, cone // EDGE, lambda h: EDGE - h, lambda h: h, between=write_stress)
+    sweep(field, outs, start, cone // EDGE, lambda h: EDGE - h, lambda h: h, between=write_stress, unroll=True)
     for copy in late[:2]:
         copy.start()
     for copy in early + late:
@@ -619,8 +657,7 @@
     tall = rows + 2 * TOP
     f32 = jnp.float32
     events = (rows - 2 * EDGE - FINAL - sum(TAIL)) // CHUNK
-    pieces = rows // CHUNK
-    slots = 2 * pieces + 3 + events + len(TAIL)
+    slots = len(LEFT) + len(RIGHT) + 3 + events // PAIR + len(TAIL)
     anywhere = pl.BlockSpec(memory_space=pl.ANY)
     vmem = pl.BlockSpec(memory_space=pltpu.VMEM)
     state = (pltpu.VMEM((FIELDS, tiles + 1, tall, LANES), f32),) + tuple(
@@ -647,13 +684,14 @@
             pltpu.VMEM((rows // FOLD, LANES), f32),
             pltpu.VMEM((rows // FOLD, LANES), f32),
             pltpu.VMEM((rows // FOLD, LANES), f32),
-            pltpu.SemaphoreType.DMA((14,)),
+            pltpu.SemaphoreType.DMA((17,)),
             pltpu.SemaphoreType.DMA((8 * tiles,)),
             pltpu.SemaphoreType.DMA((slots,)),
             pltpu.SemaphoreType.DMA((slots,)),
             pltpu.SemaphoreType.DMA((8,)),
             pltpu.SemaphoreType.DMA((8,)),
             pltpu.SemaphoreType.REGULAR,
+            pltpu.SemaphoreType.REGULAR((2,)),
         ],
         compiler_params=pltpu.CompilerParams(
             collective_id=0, has_side_effects=True, vmem_limit_bytes=44 * 2**20

time: 52.3 us -> 50.9 us (0.973)
  Pallas kernels: 51.4 us -> 50.1 us
    pallas_call x1, Pallas kernels: 49.3 us -> 48.2 us  [shards(): pl.pallas_call(functools.partial(kernel, lat_count, lon_count), out_shape...]
where the time goes in v2:
time: 50.9 us; the launch traced here: 50.7 us
  Pallas kernels  50.1 us (98%)
  between operations  0.64 us (1%)
    pallas_call x1, Pallas kernels, shards(): pl.pallas_call(functools.partial(kernel, lat_count, lon_count), out_shape...  48.2 us
    pallas_call x1, Pallas kernels, shards(): pl.pallas_call(finish, out_shape=tuple((jax.ShapeDtypeStruct((rows, cols)...  1.86 us

profile of v2, /device:TPU:1, one launch (start us, length us, event | category | flops | bytes accessed | tf_op | source)
XLA Modules:
  0.0 50.7 jit_solution(14950216239779700241)
XLA Ops:
  0.6 48.2 %ice.1 = (f32[12,6,288,128]{3,2,1,0:T(8,128)S(1)}, f32[256,640]{1,0:T(8,128)S(1)}, f32[256,640]{1,0:T(8,128)S(1)}, f32[256,640]{1,0:T(8,128)S(1)}, f32[256,640]{1,0:T(8,128)S(1)}, /*index=5*/f32[256,640]{1,0:T(8,128)S(1)}) custom-call(f32[20]{0:T(128)} %weight_hbm.1, bf16[20,256,640]{2,1,0:T(8,128)(2,1)} %thick_hbm.1, bf16[20,256,640]{2,1,0:T(8,128)(2,1)} %area_hbm.1, ...), custom_call_target="tpu_custom_call" | custom-call | tf_op jit(solution)/shard_map/ice/pallas_call | solution.py:666
  48.9 1.9 %finish.1 = (f32[256,640]{1,0:T(8,128)}, f32[256,640]{1,0:T(8,128)}, f32[256,640]{1,0:T(8,128)}, f32[256,640]{1,0:T(8,128)}, f32[256,640]{1,0:T(8,128)}, /*index...) custom-call(f32[12,6,288,128]{3,2,1,0:T(8,128)S(1)} %get-tuple-eleme, ...), custom_call_target="tpu_custom_call", output_to_operand_aliasing={{5}: (0, {}), {6}: (1, {}), {7}: (2, {}), {8}: (3, {}), {9}... | custom-call | tf_op jit(solution)/shard_map/finish/pallas_call | solution.py:715

commit v3 on v2

--- a/solution.py
+++ b/solution.py
@@ -15,8 +15,8 @@
 TAIL = (16, 16)
 FINAL = 16
 TOP = 16
-LEFT = (16, 48, 64, 128)
-RIGHT = (128, 128)
+LEFT = (16, 48, 192)
+RIGHT = (256,)
 PAIR = 1
 FOLD = 4
 MESH = pl.DeviceIdType.MESH
@@ -251,7 +251,7 @@
     load(0)
     weight_load = pltpu.make_async_copy(weight_hbm, weight, load_sem.at[16])
     weight_load.start()
-    load(1)
+    load(1, 2)
 
     has_west = my_lon > 0
     has_east = my_lon < lon_count - 1
@@ -344,7 +344,6 @@
 
     weight_load.wait()
     loaded(0)
-    load(2)
     partial(0, LEFT[0] // BLOCK, 0, 1)
     pl.semaphore_wait(barrier, before)
     strip(0).start()

time: 50.9 us -> 50.7 us (level)
  no operation moved by 1% of the time
where the time goes in v3:
time: 50.7 us; the launch traced here: 50.5 us
  Pallas kernels  49.8 us (98%)
  between operations  0.64 us (1%)
    pallas_call x1, Pallas kernels, shards(): pl.pallas_call(functools.partial(kernel, lat_count, lon_count), out_shape...  48 us
    pallas_call x1, Pallas kernels, shards(): pl.pallas_call(finish, out_shape=tuple((jax.ShapeDtypeStruct((rows, cols)...  1.86 us

profile of v3, /device:TPU:1, one launch (start us, length us, event | category | flops | bytes accessed | tf_op | source)
XLA Modules:
  0.0 50.5 jit_solution(13487236601774655593)
XLA Ops:
  0.6 48.0 %ice.1 = (f32[12,6,288,128]{3,2,1,0:T(8,128)S(1)}, f32[256,640]{1,0:T(8,128)S(1)}, f32[256,640]{1,0:T(8,128)S(1)}, f32[256,640]{1,0:T(8,128)S(1)}, f32[256,640]{1,0:T(8,128)S(1)}, /*index=5*/f32[256,640]{1,0:T(8,128)S(1)}) custom-call(f32[20]{0:T(128)} %weight_hbm.1, bf16[20,256,640]{2,1,0:T(8,128)(2,1)} %thick_hbm.1, bf16[20,256,640]{2,1,0:T(8,128)(2,1)} %area_hbm.1, ...), custom_call_target="tpu_custom_call" | custom-call | tf_op jit(solution)/shard_map/ice/pallas_call | solution.py:665
  48.6 1.9 %finish.1 = (f32[256,640]{1,0:T(8,128)}, f32[256,640]{1,0:T(8,128)}, f32[256,640]{1,0:T(8,128)}, f32[256,640]{1,0:T(8,128)}, f32[256,640]{1,0:T(8,128)}, /*index...) custom-call(f32[12,6,288,128]{3,2,1,0:T(8,128)S(1)} %get-tuple-eleme, ...), custom_call_target="tpu_custom_call", output_to_operand_aliasing={{5}: (0, {}), {6}: (1, {}), {7}: (2, {}), {8}: (3, {}), {9}... | custom-call | tf_op jit(solution)/shard_map/finish/pallas_call | solution.py:714
